TPU v7x, 32 devices: a whole 2x2x4 slice. The times are simulated.
32 devices in a mesh: dp: 8 (over z, x), mp: 4 (over y, core).
Axes of the slice: x: 2, y: 2, z: 4, core: 2. Of those that a mesh axis runs over, the one named last changes fastest.
Arguments:
- q_latent: bfloat16 [2048, 2, 768], P('dp', None, 'mp'), may hold values from -6 to 6
- kv_latent: bfloat16 [2048, 2, 256], P('dp', None, 'mp'), may hold values from -6 to 6
- q_head_grad: bfloat16 [2048, 512], P('dp'), may hold values from -0.1875 to 0.1875
- k_head_grad: bfloat16 [2048, 512], P('dp'), may hold values from -0.1875 to 0.1875
- q_heads: bfloat16 [2048, 512], P('dp', 'mp'), may hold values from -6 to 6
- k_heads: bfloat16 [2048, 512], P('dp', 'mp'), may hold values from -6 to 6
- query_pick: int32 [8, 16, 4], P('dp', None, 'mp'), may hold values from 0 to 255
- key_pick: int32 [8, 16, 4], P('dp', None, 'mp'), may hold values from 0 to 255
- q_weight: float32 [8, 768, 128], P('dp', 'mp'), may hold values from -6 to 6
- k_weight: float32 [8, 256, 128], P('dp', 'mp'), may hold values from -6 to 6
- q_moment: float32 [8, 768, 128], P('dp', 'mp'), may hold values from -6 to 6
- k_moment: float32 [8, 256, 128], P('dp', 'mp'), may hold values from -6 to 6
Outputs:
- q_weight_new: float32 [8, 768, 128], P('dp', 'mp')
- k_weight_new: float32 [8, 256, 128], P('dp', 'mp')
- q_moment_new: float32 [8, 768, 128], P('dp', 'mp')
- k_moment_new: float32 [8, 256, 128], P('dp', 'mp')
Inputs may be any that keep to these rules, and one draw needn't show every extreme that they name: `query_pick`: the index of a token among the 256 tokens of its own block b. `key_pick`: the index of a token among the 256 tokens of its own block b.
All inputs are finite; a program needn't handle non-finite values.
Results may differ from a plain program's by a relative error of at most 0.0003.
Values sent between devices are 32-bit elements; how exact they have to be, the bound alone decides.
A program may use at most 64 MiB of HBM per device.

v0:
```python
import math

import jax
import jax.numpy as jnp
from jax import lax
from jax.sharding import PartitionSpec as P

QR = 1536
KR = 512
ITERS = 5


MOMENTUM = 0.95
STEP_SIZE = 1.0
DECAY = 0.1
CLIP_LEVEL = 0.1
SCORE_SCALE = 1.0 / math.sqrt(192.0)
COEFF_A = 3.4445
COEFF_B = -4.775
COEFF_C = 2.0315
HIGHEST = lax.Precision.HIGHEST


def from_behind(value, axis, steps):
    count = lax.axis_size(axis)
    pairs = [(source, (source + steps) % count) for source in range(count)]
    return lax.ppermute(value, axis, pairs)


def gramian(matrix):
    return jnp.einsum("rc,rd->cd", matrix, matrix, precision=HIGHEST)


def unchanged(stacked):
    return stacked


def polar_steps(q_rows_in, k_rows_in, combine):
    grams = combine(jnp.stack([gramian(q_rows_in), gramian(k_rows_in)]))
    scale = 1.0 / jnp.sqrt(jnp.trace(grams, axis1=1, axis2=2) + 1.0)
    current = [q_rows_in * scale[0], k_rows_in * scale[1]]
    grams = grams * (scale * scale)[:, None, None]
    for step in range(ITERS):
        updated = []
        for member in range(2):
            square = jnp.dot(grams[member], grams[member], precision=HIGHEST)
            mixer = COEFF_B * grams[member] + COEFF_C * square
            updated.append(
                COEFF_A * current[member] + jnp.dot(current[member], mixer, precision=HIGHEST)
            )
        current = updated
        if step + 1 < ITERS:
            grams = combine(jnp.stack([gramian(current[0]), gramian(current[1])]))
    return (current[0], current[1])


def local(
    q_latent,
    kv_latent,
    q_head_grad,
    k_head_grad,
    q_heads,
    k_heads,
    query_pick,
    key_pick,
    q_weight,
    k_weight,
    q_moment,
    k_moment,
):
    head_count = lax.axis_size("dp") // 2
    tokens_here = q_latent.shape[0]
    q_rows = q_latent.shape[2]
    k_rows = kv_latent.shape[2]
    row_count = q_rows + k_rows
    width = q_moment.shape[2]
    q_grads = q_head_grad.reshape(tokens_here, head_count, width)
    k_grads = k_head_grad.reshape(tokens_here, head_count, width)
    slot_count = lax.axis_size("dp") * row_count // row_count
    slot_ids = jnp.arange(slot_count, dtype=jnp.int32)
    halves = slot_ids // head_count
    owners = slot_ids % head_count
    q_side = jnp.take(q_latent, halves, axis=1)
    k_side = jnp.take(kv_latent, halves, axis=1)
    q_cols = jnp.take(q_grads, owners, axis=1)
    k_cols = jnp.take(k_grads, owners, axis=1)
    q_term = jnp.einsum("tnr,tnc->nrc", q_side, q_cols, preferred_element_type=jnp.float32)
    k_term = jnp.einsum("tnr,tnc->nrc", k_side, k_cols, preferred_element_type=jnp.float32)
    own_term = lax.psum_scatter(
        jnp.concatenate([q_term, k_term], axis=1).reshape(lax.axis_size("dp") * row_count, width),
        "dp",
        scatter_dimension=0,
        tiled=True,
    )
    q_moment_new = MOMENTUM * q_moment[0] + own_term[:q_rows]
    k_moment_new = MOMENTUM * k_moment[0] + own_term[q_rows:]
    local_heads = query_pick.shape[2]
    q_cube = q_heads.reshape(tokens_here, local_heads, width)
    k_cube = k_heads.reshape(tokens_here, local_heads, width)
    picked_q = jnp.take_along_axis(q_cube, query_pick[0][:, :, None], axis=0)
    picked_k = jnp.take_along_axis(k_cube, key_pick[0][:, :, None], axis=0)
    scores = (
        jnp.sum(picked_q.astype(jnp.float32) * picked_k.astype(jnp.float32), axis=2) * SCORE_SCALE
    )
    local_peak = jnp.max(scores, axis=0)
    filled = jnp.full((head_count,), -1e30, jnp.float32)
    filled = lax.dynamic_update_slice(filled, local_peak, (lax.axis_index("mp") * local_heads,))
    peaks = lax.pmax(filled, ("dp", "mp"))
    own_head = lax.axis_index("dp") % head_count
    peak = lax.dynamic_index_in_dim(peaks, own_head, keepdims=False)
    shrink = jnp.sqrt(CLIP_LEVEL / jnp.maximum(peak, CLIP_LEVEL))
    q_half, k_half = (
        lax.all_gather(q_moment_new, "mp", axis=0, tiled=True),
        lax.all_gather(k_moment_new, "mp", axis=0, tiled=True),
    )
    place = lax.axis_index("mp")
    q_len = q_half.shape[0]
    k_len = k_half.shape[0]
    joined = jnp.concatenate([q_half, k_half], axis=0)
    other = from_behind(joined, "dp", lax.axis_size("dp") // 2)
    q_other = other[:q_len]
    k_other = other[q_len:]
    first = lax.axis_index("dp") < head_count
    q_full = jnp.concatenate(
        [jnp.where(first, q_half, q_other), jnp.where(first, q_other, q_half)], axis=0
    )
    k_full = jnp.concatenate(
        [jnp.where(first, k_half, k_other), jnp.where(first, k_other, k_half)], axis=0
    )
    q_whole, k_whole = polar_steps(q_full, k_full, unchanged)
    second = jnp.where(first, 0, 1).astype(jnp.int32)
    q_ortho = lax.dynamic_slice_in_dim(q_whole, second * q_len + place * q_rows, q_rows, 0)
    k_ortho = lax.dynamic_slice_in_dim(k_whole, second * k_len + place * k_rows, k_rows, 0)
    keep = 1.0 - STEP_SIZE * DECAY
    q_weight_new = (q_weight[0] * keep - STEP_SIZE * 0.2 * math.sqrt(QR) * q_ortho) * shrink
    k_weight_new = (k_weight[0] * keep - STEP_SIZE * 0.2 * math.sqrt(KR) * k_ortho) * shrink
    return (q_weight_new[None], k_weight_new[None], q_moment_new[None], k_moment_new[None])


def solution(mesh):
    in_specs = (
        P("dp", None, "mp"),
        P("dp", None, "mp"),
        P("dp", None),
        P("dp", None),
        P("dp", "mp"),
        P("dp", "mp"),
        P("dp", None, "mp"),
        P("dp", None, "mp"),
        P("dp", "mp", None),
        P("dp", "mp", None),
        P("dp", "mp", None),
        P("dp", "mp", None),
    )
    out_specs = (P("dp", "mp", None), P("dp", "mp", None), P("dp", "mp", None), P("dp", "mp", None))
    return jax.shard_map(local, mesh=mesh, in_specs=in_specs, out_specs=out_specs, check_vma=False)
```

profile of v0, /device:TPU:0, one launch (start us, length us, event | category | flops | bytes accessed | tf_op | source)
XLA Modules:
  0.0 171.6 jit_solution(16196970710219350173)
XLA Ops:
  7.3 1.1 copy.16
  8.6 0.8 copy-done.3
  9.6 0.7 gather_fusion.2
  10.3 0.6 gather_fusion.3
  11.0 0.6 gather_fusion
  13.1 1.0 pad_maximum_fusion
  14.2 0.6 copy-done.11
  16.2 65.1 %reduce-scatter.2.cloned.1.call-done = f32[256,128]{1,0:T(8,128)} async-done(((f32[2048,128]{1,0:T(8,128)}), f32[256,128]{1,0:T(8,128)}) %reduce-scatter.2.cloned.1.call-update) | async-done | bytes 131088 | tf_op jit(solution)/shard_map/reduce_scatter | solution.py:89
  81.3 0.9 slice_add_fusion
  82.2 6.6 %all_gather.6 = f32[768,128]{1,0:T(8,128)S(1)} all-gather(f32[192,128]{1,0:T(8,128)S(1)} %slice_add_fusion), channel_id=1, replica_groups=mesh['dp'=8,'mp'=4] {'mp'}, dimensions={0}, use_global_device_ids=true | all-gather | bytes 491520 | tf_op jit(solution)/shard_map/all_gather | solution.py:113
  88.7 0.8 slice_add_fusion.1
  89.5 5.4 %all_gather.7 = f32[256,128]{1,0:T(8,128)S(1)} all-gather(f32[64,128]{1,0:T(8,128)S(1)} %slice_add_fusion.1), channel_id=1, replica_groups=mesh['dp'=8,'mp'=4] {'mp'}, dimensions={0}, use_global_device_ids=true | all-gather | bytes 163840 | tf_op jit(solution)/shard_map/all_gather | solution.py:114
  95.0 1.4 collective-permute-start
  96.6 0.6 multiply_reduce_fusion.1
  97.2 0.8 dynamic_update_slice.3
  98.0 43.5 %pmax.7 = f32[4]{0:T(128)S(1)} all-reduce(f32[4]{0:T(128)S(1)} %dynamic_update_slice.3), channel_id=1, replica_groups=mesh['dp'=8,'mp'=4] {'dp','mp'}, use_global_device_ids=true, to_apply=%region_4.7 | all-reduce | flops 4 | bytes 32 | tf_op jit(solution)/shard_map/pmax | solution.py:108
  142.9 1.4 convolution_bitcast_fusion
  144.3 0.6 convolution_bitcast_fusion.1
  146.2 1.0 convolution_add_fusion.7
  147.2 0.6 fusion.57
  149.5 0.6 fusion.59
  151.9 1.4 convolution_add_fusion.3
  153.3 1.4 fusion.52
  155.0 0.8 convolution_add_fusion.2
  155.7 1.4 fusion.53
  157.4 1.0 convolution_add_fusion.1
  158.4 1.4 fusion.54
  160.0 0.8 convolution_add_fusion
  160.8 1.4 fusion.55
  162.4 0.8 fusion.56
  163.2 0.6 fusion.40
  164.1 0.7 fusion.36
  (71 shorter events, 10.1 us)
Async XLA Ops:
  7.2 3.8 %copy-start = (bf16[256,2,192]{0,2,1:T(8,128)(2,1)S(1)}, bf16[256,2,192]{0,2,1:T(8,128)(2,1)}, u32[]{:S(2)}) copy-start(bf16[256,2,192]{0,2,1:T(8,128)(2,1)} %param.16) | copy-start | bytes 589828
  7.2 74.1 %reduce-scatter.2.cloned.1.call-start = ((), (), s32[]{:S(2)}) async-start(), calls=%async_computation.1 | async-start | bytes 1179648 | tf_op jit(solution)/shard_map/reduce_scatter | solution.py:89
  8.4 1.0 copy-start.3
  11.0 0.8 copy-start.1
  14.1 0.7 copy-start.11
  14.2 0.7 copy-start.12
  14.2 0.9 copy-start.9
  14.2 1.5 copy-start.10
  14.2 67.1 %copy-start.5 = (f32[1,192,128]{2,1,0:T(8,128)S(1)}, f32[1,192,128]{2,1,0:T(8,128)}, u32[]{:S(2)}) copy-start(f32[1,192,128]{2,1,0:T(8,128)} %param.26) | copy-start | bytes 294916
  82.2 6.6 %copy-start.2 = (f32[192,128]{1,0:T(8,128)}, f32[192,128]{1,0:T(8,128)S(1)}, u32[]{:S(2)}) copy-start(f32[192,128]{1,0:T(8,128)S(1)} %slice_add_fusion) | copy-start | bytes 294916
  82.2 6.6 %copy-start.7 = (f32[1,64,128]{2,1,0:T(8,128)S(1)}, f32[1,64,128]{2,1,0:T(8,128)}, u32[]{:S(2)}) copy-start(f32[1,64,128]{2,1,0:T(8,128)} %param.27) | copy-start | bytes 98308
  89.5 5.4 %copy-start.4 = (f32[64,128]{1,0:T(8,128)}, f32[64,128]{1,0:T(8,128)S(1)}, u32[]{:S(2)}) copy-start(f32[64,128]{1,0:T(8,128)S(1)} %slice_add_fusion.1) | copy-start | bytes 98308
  95.0 47.8 %collective-permute-start = (f32[1024,128]{1,0:T(8,128)S(1)}, f32[1024,128]{1,0:T(8,128)S(1)}, u32[]{:S(2)}, u32[]{:S(2)}) collective-permute-start(f32[1024,128]{1,0:T(8,128)S(1)} %pad_maximum_fusion.4), channel_id=1, source_target_pairs={{0,16},{4,20},{8,24},{12,28},{16,0},{20,4},{24,8},{28,12},{1,17},{... | collective-permute-start | bytes 1572872 | tf_op jit(solution)/shard_map/ppermute | solution.py:27
  162.4 0.8 copy-start.8
  163.2 0.9 copy-start.6
Sparse Core Ops, SparseCore 0:
  14.3 66.8 reduce-scatter.1
where the time goes:
time: 172 us
  waiting for transfers between devices  65.1 us (38%)
  blocking collectives  55.4 us (32%)
  matrix products  20 us (12%)
  between operations  15.3 us (9%)
  local copies, waits for them, and re-layouts  9.17 us (5%)
  other arithmetic  5.2 us (3%)
    reduce_scatter x1, waiting for transfers between devices, local(): lax.psum_scatter(jnp.concatenate([q_term, k_term], axis=1).reshape(lax.ax...  65.1 us
    pmax x1, blocking collectives, local(): peaks = lax.pmax(filled, ('dp', 'mp'))  43.5 us
    dot_general x10, matrix products, gramian(): return jnp.einsum('rc,rd->cd', matrix, matrix, precision=HIGHEST)  10 us
    dot_general x10, matrix products, polar_steps(): jnp.dot(current[member], mixer, precision=HIGHEST)  7.19 us
    all_gather x1, blocking collectives, local(): lax.all_gather(q_moment_new, 'mp', axis=0, tiled=True)  6.55 us
    all_gather x1, blocking collectives, local(): lax.all_gather(k_moment_new, 'mp', axis=0, tiled=True)  5.41 us
  transfers between devices with their start and end apart: 2, of which 1 were waited for; matrix products, arithmetic and copies ran while one was open for 2% of the time, Pallas kernels for 0%

commit v1 on v0

v1 whole, which is shorter than its diff:
```python
import functools
import math

import jax
import jax.numpy as jnp
from jax import lax
from jax.experimental import pallas as pl
from jax.experimental.pallas import tpu as pltpu
from jax.sharding import PartitionSpec as P

ITERS = 5
MOMENTUM = 0.95
STEP_SIZE = 1.0
DECAY = 0.1
CLIP_LEVEL = 0.1
SCORE_SCALE = 1.0 / math.sqrt(192.0)
COEFF_A = 3.4445
COEFF_B = -4.775
COEFF_C = 2.0315
LOWEST = -1e30
MESH = pl.DeviceIdType.MESH
F32 = jnp.float32
BF16 = jnp.bfloat16


def split(value):
    high = value.astype(BF16)
    return high, (value - high.astype(F32)).astype(BF16)


def mm(a, b):
    return jnp.dot(a, b, preferred_element_type=F32)


def mm3(a, b):
    return mm(a[0], b[0]) + (mm(a[0], b[1]) + mm(a[1], b[0]))


def gram(rows):
    high, low = split(rows)
    high_t = high.T
    cross = mm(high_t, low)
    return mm(high_t, high) + (cross + cross.T)


def partner(index, count, step):
    if count & (count - 1):
        return lax.rem(index + step, count)
    result = 0
    bit = 1
    while bit < count:
        held = lax.rem(lax.div(index, bit), 2)
        result = result + bit * ((1 - held) if step & bit else held)
        bit *= 2
    return result


def kernel(
    n_dp, n_mp, heads,
    lat_ref, qg_ref, kg_ref, qh_ref, kh_ref, qp_ref, kp_ref, qw_ref, kw_ref, qm_ref, km_ref,
    qw_out, kw_out, qm_out, km_out,
    near_send, near_recv, own, far_recv, peak_send, peak_recv, peak2_send, peak2_recv,
    grams, gram_recv, row_send, row_recv, z_send, z_recv, mix,
    ns_s, ns_r, fs_s, fs_r, pk_s, pk_r, pm_s, pm_r, g_s, g_r, y_s, y_r, z_s, z_r, m_s, m_r,
):
    dp = lax.axis_index("dp")
    mp = lax.axis_index("mp")
    n_outer = n_dp // 2
    outer = lax.div(dp, 2)
    inner = lax.rem(dp, 2)
    core = lax.rem(mp, 2)
    group = lax.div(mp, 2)
    n_group = n_mp // 2
    q_rows = qm_ref.shape[1]
    k_rows = km_ref.shape[1]
    width = qm_ref.shape[2]
    tokens = qg_ref.shape[0]
    other_core = mp + 1 - 2 * core

    barrier = pltpu.get_barrier_semaphore()
    for step in range(1, n_dp):
        pl.semaphore_signal(
            barrier, inc=1, device_id=(lax.rem(dp + step, n_dp), mp), device_id_type=MESH
        )
    for step in range(1, n_mp):
        pl.semaphore_signal(
            barrier, inc=1, device_id=(dp, lax.rem(mp + step, n_mp)), device_id_type=MESH
        )

    def copy(src, dst, send, recv, where):
        return pltpu.make_async_remote_copy(
            src_ref=src, dst_ref=dst, send_sem=send, recv_sem=recv,
            device_id=where, device_id_type=MESH,
        )

    def term(dst, where, to_outer, to_inner):
        slot = 2 * to_outer + to_inner
        half = lax.div(slot, heads)
        cols = pl.ds(pl.multiple_of(lax.rem(slot, heads) * width, width), width)
        dst[where, :q_rows, :] = mm(lat_ref[half, :q_rows, :], qg_ref[:, cols])
        dst[where, q_rows:, :] = mm(lat_ref[half, q_rows:, :], kg_ref[:, cols])

    order = list(range(n_outer - 1, -1, -1))
    neighbour = (dp + 1 - 2 * inner, mp)
    near = []
    for spot, step in enumerate(order):
        term(near_send, spot, partner(outer, n_outer, step), 1 - inner)
        if spot == 0:
            pl.semaphore_wait(barrier, n_dp + n_mp - 2)
        each = copy(near_send.at[spot], near_recv.at[spot], ns_s.at[spot], ns_r.at[spot], neighbour)
        each.start()
        near.append(each)

    local_heads = qp_ref.shape[2]
    lane = lax.broadcasted_iota(jnp.int32, (8, width), 1)
    peaks = jnp.full((8, width), LOWEST, F32)
    ids = lax.broadcasted_iota(jnp.int32, (qp_ref.shape[1], tokens), 1)
    for head in range(local_heads):
        span = slice(head * width, (head + 1) * width)
        pick_q = (ids == qp_ref[0, :, head : head + 1]).astype(F32).astype(BF16)
        pick_k = (ids == kp_ref[0, :, head : head + 1]).astype(F32).astype(BF16)
        score = jnp.sum(
            mm(pick_q, qh_ref[:, span]) * mm(pick_k, kh_ref[:, span]), axis=1, keepdims=True
        )
        top = jnp.max(score * SCORE_SCALE, axis=0, keepdims=True)
        peaks = jnp.where(lane == mp * local_heads + head, top, peaks)
    peak_send[...] = peaks
    peak_copies = []
    for step in range(1, n_dp):
        each = copy(
            peak_send, peak_recv.at[step - 1], pk_s.at[step - 1], pk_r.at[step - 1],
            (lax.rem(dp + step, n_dp), mp),
        )
        each.start()
        peak_copies.append(each)

    for spot, step in enumerate(order):
        term(own, spot, partner(outer, n_outer, step), inner)
    far = []
    for spot, step in enumerate(order):
        near[spot].wait_recv()
        if step:
            own[spot] = own[spot] + near_recv[spot]
            each = copy(
                own.at[spot], far_recv.at[spot], fs_s.at[spot], fs_r.at[spot],
                (2 * partner(outer, n_outer, step) + inner, mp),
            )
            each.start()
            far.append(each)
    last = n_outer - 1
    total = own[last] + near_recv[last]

    for each in peak_copies:
        each.wait_recv()
    peaks = jnp.maximum(peaks, jnp.max(peak_recv[...], axis=0))
    peak2_send[...] = peaks
    peak2_copies = []
    for step in range(1, n_mp):
        each = copy(
            peak2_send, peak2_recv.at[step - 1], pm_s.at[step - 1], pm_r.at[step - 1],
            (dp, lax.rem(mp + step, n_mp)),
        )
        each.start()
        peak2_copies.append(each)

    for spot in range(last):
        far[spot].wait_recv()
        total = total + far_recv[spot]
    q_moment = MOMENTUM * qm_ref[0] + total[:q_rows]
    k_moment = MOMENTUM * km_ref[0] + total[q_rows:]
    qm_out[0] = q_moment
    km_out[0] = k_moment

    grams[0] = gram(q_moment)
    grams[1] = gram(k_moment)
    swap = copy(grams.at[1 - core], gram_recv, g_s, g_r, (dp, other_core))
    swap.start()
    swap.wait_recv()
    whole = grams[core] + gram_recv[...]
    rows = []
    if n_group > 1:
        row_send[...] = whole
        for step in range(1, n_group):
            each = copy(
                row_send, row_recv.at[step - 1], y_s.at[step - 1], y_r.at[step - 1],
                (dp, 2 * lax.rem(group + step, n_group) + core),
            )
            each.start()
            rows.append(each)
        for step in range(1, n_group):
            rows[step - 1].wait_recv()
            whole = whole + row_recv[step - 1]
    z_send[...] = whole
    cross = copy(z_send, z_recv, z_s, z_r, (lax.rem(dp + heads, n_dp), mp))
    cross.start()
    cross.wait_recv()
    whole = whole + z_recv[...]

    eye = (
        lax.broadcasted_iota(jnp.int32, (width, width), 0)
        == lax.broadcasted_iota(jnp.int32, (width, width), 1)
    ).astype(F32)
    trace = jnp.sum(jnp.sum(whole * eye, axis=0, keepdims=True), axis=1, keepdims=True)
    scale = 1.0 / jnp.sqrt(trace + 1.0)
    current = whole * (scale * scale)
    mixed = None
    for step in range(ITERS):
        parts = split(current)
        square = mm3(parts, parts)
        poly = COEFF_A * eye + COEFF_B * current + COEFF_C * square
        pair = split(poly)
        mixed = poly * scale if mixed is None else mm3(split(mixed), pair)
        if step + 1 < ITERS:
            current = mm3(split(mm3(parts, pair)), pair)
    mix[core] = mixed
    swap2 = copy(mix.at[core], mix.at[core], m_s, m_r, (dp, other_core))
    swap2.start()

    for each in peak2_copies:
        each.wait_recv()
    peaks = jnp.maximum(peaks, jnp.max(peak2_recv[...], axis=0))
    mine = jnp.where(lane == lax.rem(dp, heads), peaks, LOWEST)
    peak = jnp.max(jnp.max(mine, axis=0, keepdims=True), axis=1, keepdims=True)
    shrink = jnp.sqrt(CLIP_LEVEL / jnp.maximum(peak, CLIP_LEVEL))
    keep = 1.0 - STEP_SIZE * DECAY
    q_full = q_rows * n_mp * 2
    k_full = k_rows * n_mp * 2
    q_parts = split(q_moment)
    k_parts = split(k_moment)
    swap2.wait_recv()
    q_ortho = mm3(q_parts, split(mix[0]))
    k_ortho = mm3(k_parts, split(mix[1]))
    qw_out[0] = (qw_ref[0] * keep - (STEP_SIZE * 0.2 * math.sqrt(q_full)) * q_ortho) * shrink
    kw_out[0] = (kw_ref[0] * keep - (STEP_SIZE * 0.2 * math.sqrt(k_full)) * k_ortho) * shrink
    for each in near + far + peak_copies + peak2_copies + [swap] + rows + [cross, swap2]:
        each.wait_send()


def local(
    q_latent, kv_latent, q_head_grad, k_head_grad, q_heads, k_heads,
    query_pick, key_pick, q_weight, k_weight, q_moment, k_moment,
):
    n_dp = lax.axis_size("dp")
    n_mp = lax.axis_size("mp")
    heads = n_dp // 2
    n_outer = n_dp // 2
    n_group = max(n_mp // 2, 2)
    rows = q_latent.shape[2] + kv_latent.shape[2]
    width = q_moment.shape[2]
    latent = jnp.concatenate([q_latent, kv_latent], axis=2).transpose(1, 2, 0)
    vmem = pltpu.VMEM
    dma = pltpu.SemaphoreType.DMA
    square = (width, width)
    tile = (8, width)
    return pl.pallas_call(
        functools.partial(kernel, n_dp, n_mp, heads),
        out_shape=[jax.ShapeDtypeStruct(a.shape, F32) for a in (q_weight, k_weight, q_moment, k_moment)],
        in_specs=[pl.BlockSpec(memory_space=vmem)] * 11,
        out_specs=[pl.BlockSpec(memory_space=vmem)] * 4,
        scratch_shapes=[
            vmem((n_outer, rows, width), F32),
            vmem((n_outer, rows, width), F32),
            vmem((n_outer, rows, width), F32),
            vmem((n_outer, rows, width), F32),
            vmem(tile, F32),
            vmem((n_dp - 1,) + tile, F32),
            vmem(tile, F32),
            vmem((n_mp - 1,) + tile, F32),
            vmem((2,) + square, F32),
            vmem(square, F32),
            vmem(square, F32),
            vmem((n_group - 1,) + square, F32),
            vmem(square, F32),
            vmem(square, F32),
            vmem((2,) + square, F32),
            dma((n_outer,)), dma((n_outer,)),
            dma((n_outer,)), dma((n_outer,)),
            dma((n_dp - 1,)), dma((n_dp - 1,)),
            dma((n_mp - 1,)), dma((n_mp - 1,)),
            dma, dma,
            dma((n_group - 1,)), dma((n_group - 1,)),
            dma, dma,
            dma, dma,
        ],
        compiler_params=pltpu.CompilerParams(
            collective_id=0, has_side_effects=True, vmem_limit_bytes=56 * 1024 * 1024
        ),
    )(
        latent, q_head_grad, k_head_grad, q_heads, k_heads,
        query_pick, key_pick, q_weight, k_weight, q_moment, k_moment,
    )


def solution(mesh):
    rows3 = P("dp", "mp", None)
    in_specs = (
        P("dp", None, "mp"), P("dp", None, "mp"), P("dp", None), P("dp", None),
        P("dp", "mp"), P("dp", "mp"), P("dp", None, "mp"), P("dp", None, "mp"),
        rows3, rows3, rows3, rows3,
    )
    return jax.shard_map(
        lambda *args: tuple(local(*args)),
        mesh=mesh, in_specs=in_specs, out_specs=(rows3,) * 4, check_vma=False,
    )
```

time: 172 us -> 43.2 us (0.25)
  the two profiles are of different devices: /device:TPU:0 before, /device:TPU:9 now
where the time goes in v1:
time: 43.2 us; the launch traced here: 42.9 us
  Pallas kernels  35 us (81%)
  local copies, waits for them, and re-layouts  5.59 us (13%)
  other arithmetic  1.67 us (4%)
  between operations  0.67 us (2%)
    pallas_call x1, Pallas kernels, local(): pl.pallas_call(functools.partial(kernel, n_dp, n_mp, heads), out_shape=[j...  35 us
    unnamed x14, local copies, waits for them, and re-layouts  5.59 us
    transpose x1, other arithmetic, local(): latent = jnp.concatenate([q_latent, kv_latent], axis=2).transpose(1, 2, 0)  1.67 us

profile of v1, /device:TPU:9, one launch (start us, length us, event | category | flops | bytes accessed | tf_op | source)
XLA Modules:
  0.0 42.9 jit_solution(16410377969744781864)
XLA Ops:
  0.6 0.0 copy-start.3
  0.6 1.3 %copy.16.qp_ref = s32[1,16,1]{2,1,0:T(8,128)} copy(s32[1,16,1]{1,2,0:T(1,128)} %param.18) | data formatting | bytes 128 | tf_op args[6]
  2.0 0.0 copy-done.3
  2.0 0.7 %copy.17.kp_ref = s32[1,16,1]{2,1,0:T(8,128)} copy(s32[1,16,1]{1,2,0:T(1,128)S(1)} %copy-done.3) | data formatting | bytes 128 | tf_op args[7]
  2.7 1.7 %maximum_bitcast_fusion.lat_ref = bf16[2,256,256]{2,1,0:T(8,128)(2,1)} fusion(bf16[256,2,64]{0,2,1:T(8,128)(2,1)} %param.13, bf16[256,2,192]{0,2,1:T(8,128)(2,1)} %param.12), kind=kLoop, calls=%fused_computation | loop fusion | flops 524288 | bytes 524288 | tf_op jit(solution)/shard_map/transpose | solution.py:250
  4.3 35.0 %shard_map.147 = (f32[1,192,128]{2,1,0:T(8,128)}, f32[1,64,128]{2,1,0:T(8,128)}, f32[1,192,128]{2,1,0:T(8,128)}, f32[1,64,128]{2,1,0:T(8,128)}) custom-call(bf16[2,256,256]{2,1,0:T(8,128)(2,1)} %maximum_bitcast_fusion.lat_ref, bf16[256,512]{1,0:T(8,128)(2,1)} %qg_ref.1, bf16[256,512]{1,0:T(8,128)(2,1)} %kg_ref.1, bf16[256,128]{1,0:T(8,128)(2,1)} %qh_ref.1, ...), custom_call_target="tpu_custom_call" | custom-call | tf_op jit(solution)/shard_map/pallas_call | solution.py:255
  39.3 0.0 copy-start.2
  39.3 0.0 copy-start
  39.3 1.6 %copy.22 = f32[1,192,128]{2,1,0:T(8,128)} copy(f32[1,192,128]{2,1,0:T(8,128)} %get-tuple-element.8) | data formatting | bytes 196608
  40.9 0.0 copy-done.2
  40.9 0.6 %copy.23 = f32[1,64,128]{2,1,0:T(8,128)} copy(f32[1,64,128]{2,1,0:T(8,128)S(1)} %copy-done.2) | data formatting | bytes 65536
  41.5 0.0 copy-done
  41.5 0.0 copy-start.1
  41.5 0.6 %copy.24 = f32[1,192,128]{2,1,0:T(8,128)} copy(f32[1,192,128]{2,1,0:T(8,128)S(1)} %copy-done) | data formatting | bytes 196608
  42.2 0.1 copy-done.1
  42.3 0.6 %copy.25 = f32[1,64,128]{2,1,0:T(8,128)} copy(f32[1,64,128]{2,1,0:T(8,128)S(1)} %copy-done.1) | data formatting | bytes 65536
Async XLA Ops:
  0.6 1.3 %copy-start.3 = (s32[1,16,1]{1,2,0:T(1,128)S(1)}, s32[1,16,1]{1,2,0:T(1,128)}, u32[]{:S(2)}) copy-start(s32[1,16,1]{1,2,0:T(1,128)} %param.19) | copy-start | bytes 196
  39.3 1.6 %copy-start.2 = (f32[1,64,128]{2,1,0:T(8,128)S(1)}, f32[1,64,128]{2,1,0:T(8,128)}, u32[]{:S(2)}) copy-start(f32[1,64,128]{2,1,0:T(8,128)} %get-tuple-element.9) | copy-start | bytes 98308
  39.3 2.2 %copy-start = (f32[1,192,128]{2,1,0:T(8,128)S(1)}, f32[1,192,128]{2,1,0:T(8,128)}, u32[]{:S(2)}) copy-start(f32[1,192,128]{2,1,0:T(8,128)} %get-tuple-element.10) | copy-start | bytes 294916
  41.5 0.8 %copy-start.1 = (f32[1,64,128]{2,1,0:T(8,128)S(1)}, f32[1,64,128]{2,1,0:T(8,128)}, u32[]{:S(2)}) copy-start(f32[1,64,128]{2,1,0:T(8,128)} %get-tuple-element.11) | copy-start | bytes 98308

commit v2 on v1

--- a/solution.py
+++ b/solution.py
@@ -43,6 +43,42 @@
     return mm(high_t, high) + (cross + cross.T)
 
 
+def fold(matrix):
+    width = matrix.shape[0]
+    half = width // 2
+    row = lax.broadcasted_iota(jnp.int32, (half, width), 0)
+    lane = lax.broadcasted_iota(jnp.int32, (half, width), 1)
+    lower = matrix[half:]
+    body = jnp.where(lane >= row, matrix[:half], pltpu.roll(lower, half, 1))
+    ends = jnp.sum(jnp.where(lane == row + half, lower, 0.0), axis=0, keepdims=True)
+    return body, jnp.broadcast_to(ends, (8, width))
+
+
+def unfold(message):
+    width = message.shape[1]
+    half = width // 2
+    row = lax.broadcasted_iota(jnp.int32, (half, width), 0)
+    lane = lax.broadcasted_iota(jnp.int32, (half, width), 1)
+    body = message[:half]
+    ends = jnp.broadcast_to(message[half : half + 1], (half, width))
+    top = jnp.where(lane >= row, body, 0.0)
+    strict = jnp.where((lane >= half) & (lane - half < row), pltpu.roll(body, half, 1), 0.0)
+    one_side = jnp.concatenate([top, jnp.where(lane == row + half, ends, strict)], axis=0)
+    full_row = lax.broadcasted_iota(jnp.int32, (width, width), 0)
+    full_lane = lax.broadcasted_iota(jnp.int32, (width, width), 1)
+    return one_side + jnp.where(full_row == full_lane, 0.0, one_side.T)
+
+
+def column(row):
+    count = row.shape[1]
+    spread = jnp.broadcast_to(row, (count, count))
+    same = lax.broadcasted_iota(jnp.int32, (count, count), 0) == lax.broadcasted_iota(
+        jnp.int32, (count, count), 1
+    )
+    picked = jnp.where(same, spread, 0).astype(F32)
+    return jnp.sum(picked, axis=1, keepdims=True).astype(jnp.int32)
+
+
 def partner(index, count, step):
     if count & (count - 1):
         return lax.rem(index + step, count)
@@ -57,10 +93,11 @@
 
 def kernel(
     n_dp, n_mp, heads,
-    lat_ref, qg_ref, kg_ref, qh_ref, kh_ref, qp_ref, kp_ref, qw_ref, kw_ref, qm_ref, km_ref,
-    qw_out, kw_out, qm_out, km_out,
+    ql_in, kl_in, qg_in, kg_in, qh_in, kh_in, qp_in, kp_in, qw_in, kw_in, qm_in, km_in,
+    qw_out, kw_out, qm_out, km_out, mix, shrink_out,
+    ql_ref, kl_ref, qg_ref, kg_ref, qh_ref, kh_ref, qp_ref, kp_ref, qw_ref, kw_ref, qm_ref, km_ref, in_sems,
     near_send, near_recv, own, far_recv, peak_send, peak_recv, peak2_send, peak2_recv,
-    grams, gram_recv, row_send, row_recv, z_send, z_recv, mix,
+    grams, gram_recv, row_send, row_recv, z_send, z_recv,
     ns_s, ns_r, fs_s, fs_r, pk_s, pk_r, pm_s, pm_r, g_s, g_r, y_s, y_r, z_s, z_r, m_s, m_r,
 ):
     dp = lax.axis_index("dp")
@@ -87,6 +124,17 @@
             barrier, inc=1, device_id=(dp, lax.rem(mp + step, n_mp)), device_id_type=MESH
         )
 
+    loads = [
+        pltpu.make_async_copy(src, dst, in_sems.at[i])
+        for i, (src, dst) in enumerate((
+            (ql_in, ql_ref), (kl_in, kl_ref), (qg_in, qg_ref), (kg_in, kg_ref),
+            (qp_in, qp_ref), (kp_in, kp_ref), (qh_in, qh_ref), (kh_in, kh_ref),
+            (qm_in, qm_ref), (km_in, km_ref), (qw_in, qw_ref), (kw_in, kw_ref),
+        ))
+    ]
+    for each in loads:
+        each.start()
+
     def copy(src, dst, send, recv, where):
         return pltpu.make_async_remote_copy(
             src_ref=src, dst_ref=dst, send_sem=send, recv_sem=recv,
@@ -97,9 +145,11 @@
         slot = 2 * to_outer + to_inner
         half = lax.div(slot, heads)
         cols = pl.ds(pl.multiple_of(lax.rem(slot, heads) * width, width), width)
-        dst[where, :q_rows, :] = mm(lat_ref[half, :q_rows, :], qg_ref[:, cols])
-        dst[where, q_rows:, :] = mm(lat_ref[half, q_rows:, :], kg_ref[:, cols])
-
+        dst[where, :q_rows, :] = mm(ql_ref[half], qg_ref[:, cols])
+        dst[where, q_rows:, :] = mm(kl_ref[half], kg_ref[:, cols])
+
+    for each in loads[:4]:
+        each.wait()
     order = list(range(n_outer - 1, -1, -1))
     neighbour = (dp + 1 - 2 * inner, mp)
     near = []
@@ -111,14 +161,16 @@
         each.start()
         near.append(each)
 
-    local_heads = qp_ref.shape[2]
+    for each in loads[4:8]:
+        each.wait()
+    local_heads = qp_ref.shape[0]
     lane = lax.broadcasted_iota(jnp.int32, (8, width), 1)
     peaks = jnp.full((8, width), LOWEST, F32)
-    ids = lax.broadcasted_iota(jnp.int32, (qp_ref.shape[1], tokens), 1)
+    ids = lax.broadcasted_iota(jnp.int32, (qp_ref.shape[2], tokens), 1)
     for head in range(local_heads):
         span = slice(head * width, (head + 1) * width)
-        pick_q = (ids == qp_ref[0, :, head : head + 1]).astype(F32).astype(BF16)
-        pick_k = (ids == kp_ref[0, :, head : head + 1]).astype(F32).astype(BF16)
+        pick_q = (ids == column(qp_ref[head])).astype(F32).astype(BF16)
+        pick_k = (ids == column(kp_ref[head])).astype(F32).astype(BF16)
         score = jnp.sum(
             mm(pick_q, qh_ref[:, span]) * mm(pick_k, kh_ref[:, span]), axis=1, keepdims=True
         )
@@ -166,13 +218,18 @@
     for spot in range(last):
         far[spot].wait_recv()
         total = total + far_recv[spot]
+    for each in loads[8:]:
+        each.wait()
     q_moment = MOMENTUM * qm_ref[0] + total[:q_rows]
     k_moment = MOMENTUM * km_ref[0] + total[q_rows:]
     qm_out[0] = q_moment
     km_out[0] = k_moment
 
-    grams[0] = gram(q_moment)
-    grams[1] = gram(k_moment)
+    top = width // 2
+    for which, matrix in enumerate((gram(q_moment), gram(k_moment))):
+        body, ends = fold(matrix)
+        grams[which, :top, :] = body
+        grams[which, top:, :] = ends
     swap = copy(grams.at[1 - core], gram_recv, g_s, g_r, (dp, other_core))
     swap.start()
     swap.wait_recv()
@@ -194,7 +251,7 @@
     cross = copy(z_send, z_recv, z_s, z_r, (lax.rem(dp + heads, n_dp), mp))
     cross.start()
     cross.wait_recv()
-    whole = whole + z_recv[...]
+    whole = unfold(whole + z_recv[...])
 
     eye = (
         lax.broadcasted_iota(jnp.int32, (width, width), 0)
@@ -223,17 +280,22 @@
     peak = jnp.max(jnp.max(mine, axis=0, keepdims=True), axis=1, keepdims=True)
     shrink = jnp.sqrt(CLIP_LEVEL / jnp.maximum(peak, CLIP_LEVEL))
     keep = 1.0 - STEP_SIZE * DECAY
-    q_full = q_rows * n_mp * 2
-    k_full = k_rows * n_mp * 2
-    q_parts = split(q_moment)
-    k_parts = split(k_moment)
+    shrink_out[...] = jnp.broadcast_to(shrink, shrink_out.shape)
+    qw_out[0] = (qw_ref[0] * keep) * shrink
+    kw_out[0] = (kw_ref[0] * keep) * shrink
     swap2.wait_recv()
-    q_ortho = mm3(q_parts, split(mix[0]))
-    k_ortho = mm3(k_parts, split(mix[1]))
-    qw_out[0] = (qw_ref[0] * keep - (STEP_SIZE * 0.2 * math.sqrt(q_full)) * q_ortho) * shrink
-    kw_out[0] = (kw_ref[0] * keep - (STEP_SIZE * 0.2 * math.sqrt(k_full)) * k_ortho) * shrink
     for each in near + far + peak_copies + peak2_copies + [swap] + rows + [cross, swap2]:
         each.wait_send()
+
+
+def finish(n_mp, qw_ref, kw_ref, qm_ref, km_ref, mix_ref, shrink_ref, qw_out, kw_out, qm_out, km_out):
+    groups = ((qw_ref, qm_ref, qw_out, qm_out), (kw_ref, km_ref, kw_out, km_out))
+    for which, (weight, moment, weight_out, moment_out) in enumerate(groups):
+        rows = moment[0]
+        size = STEP_SIZE * 0.2 * math.sqrt(2 * n_mp * rows.shape[0])
+        ortho = mm3(split(rows), split(mix_ref[which]))
+        moment_out[0] = rows
+        weight_out[0] = weight[0] - (size * ortho) * shrink_ref[0:1, :]
 
 
 def local(
@@ -247,17 +309,24 @@
     n_group = max(n_mp // 2, 2)
     rows = q_latent.shape[2] + kv_latent.shape[2]
     width = q_moment.shape[2]
-    latent = jnp.concatenate([q_latent, kv_latent], axis=2).transpose(1, 2, 0)
+    operands = (
+        q_latent.transpose(1, 2, 0), kv_latent.transpose(1, 2, 0), q_head_grad, k_head_grad,
+        q_heads, k_heads, query_pick.transpose(2, 0, 1), key_pick.transpose(2, 0, 1),
+        q_weight, k_weight, q_moment, k_moment,
+    )
     vmem = pltpu.VMEM
     dma = pltpu.SemaphoreType.DMA
     square = (width, width)
+    folded = (width // 2 + 8, width)
     tile = (8, width)
-    return pl.pallas_call(
+    shapes = [a.shape for a in (q_weight, k_weight, q_moment, k_moment)]
+    parts = pl.pallas_call(
         functools.partial(kernel, n_dp, n_mp, heads),
-        out_shape=[jax.ShapeDtypeStruct(a.shape, F32) for a in (q_weight, k_weight, q_moment, k_moment)],
-        in_specs=[pl.BlockSpec(memory_space=vmem)] * 11,
-        out_specs=[pl.BlockSpec(memory_space=vmem)] * 4,
-        scratch_shapes=[
+        out_shape=[vmem(shape, F32) for shape in shapes + [(2,) + square, tile]],
+        in_specs=[pl.BlockSpec(memory_space=pl.ANY)] * 12,
+        out_specs=[pl.BlockSpec(memory_space=vmem)] * 6,
+        scratch_shapes=[vmem(a.shape, a.dtype) for a in operands] + [
+            dma((12,)),
             vmem((n_outer, rows, width), F32),
             vmem((n_outer, rows, width), F32),
             vmem((n_outer, rows, width), F32),
@@ -266,13 +335,12 @@
             vmem((n_dp - 1,) + tile, F32),
             vmem(tile, F32),
             vmem((n_mp - 1,) + tile, F32),
-            vmem((2,) + square, F32),
-            vmem(square, F32),
-            vmem(square, F32),
-            vmem((n_group - 1,) + square, F32),
-            vmem(square, F32),
-            vmem(square, F32),
-            vmem((2,) + square, F32),
+            vmem((2,) + folded, F32),
+            vmem(folded, F32),
+            vmem(folded, F32),
+            vmem((n_group - 1,) + folded, F32),
+            vmem(folded, F32),
+            vmem(folded, F32),
             dma((n_outer,)), dma((n_outer,)),
             dma((n_outer,)), dma((n_outer,)),
             dma((n_dp - 1,)), dma((n_dp - 1,)),
@@ -285,10 +353,13 @@
         compiler_params=pltpu.CompilerParams(
             collective_id=0, has_side_effects=True, vmem_limit_bytes=56 * 1024 * 1024
         ),
-    )(
-        latent, q_head_grad, k_head_grad, q_heads, k_heads,
-        query_pick, key_pick, q_weight, k_weight, q_moment, k_moment,
-    )
+    )(*operands)
+    return pl.pallas_call(
+        functools.partial(finish, n_mp),
+        out_shape=[jax.ShapeDtypeStruct(shape, F32) for shape in shapes],
+        in_specs=[pl.BlockSpec(memory_space=vmem)] * 6,
+        out_specs=[pl.BlockSpec(memory_space=vmem)] * 4,
+    )(*[pltpu.with_memory_space_constraint(part, vmem) for part in parts])
 
 
 def solution(mesh):

time: 43.2 us -> 33.8 us (0.78)
  the two profiles are of different devices: /device:TPU:9 before, /device:TPU:0 now
where the time goes in v2:
time: 33.8 us; the launch traced here: 33.3 us
  Pallas kernels  32.6 us (96%)
  between operations  0.64 us (2%)
    pallas_call x1, Pallas kernels, local(): pl.pallas_call(functools.partial(kernel, n_dp, n_mp, heads), out_shape=[v...  31.7 us
    pallas_call x1, Pallas kernels, local(): pl.pallas_call(functools.partial(finish, n_mp), out_shape=[jax.ShapeDtype...  0.9 us

profile of v2, /device:TPU:0, one launch (start us, length us, event | category | flops | bytes accessed | tf_op | source)
XLA Modules:
  0.0 33.3 jit_solution(18029527032827161930)
XLA Ops:
  0.6 31.7 %shard_map.147 = (f32[1,192,128]{2,1,0:T(8,128)S(1)}, f32[1,64,128]{2,1,0:T(8,128)S(1)}, f32[1,192,128]{2,1,0:T(8,128)S(1)}, f32[1,64,128]{2,1,0:T(8,128)S(1)}, ...) custom-call(bf16[2,192,256]{2,1,0:T(8,128)(2,1)} %bitcast.4, bf16[2,64,256]{2,1,0:T(8,128)(2,1)} %bitcast.5, ...), custom_call_target="tpu_custom_call" | custom-call | tf_op jit(solution)/shard_map/pallas_call | solution.py:323
  32.4 0.9 %shard_map.148 = (f32[1,192,128]{2,1,0:T(8,128)}, f32[1,64,128]{2,1,0:T(8,128)}, f32[1,192,128]{2,1,0:T(8,128)}, f32[1,64,128]{2,1,0:T(8,128)}) custom-call(f32[1,192,128]{2,1,0:T(8,128)S(1)} %get-tuple-element.10.qw_ref, f32[1,64,128]{2,1,0:T(8,128)S(1)} %get-tuple-element.11.kw_ref, f32[1,192,128]{2,1,0:T(8,128)S(1)} %get-tuple-element.12.qm_ref, ...), custom_call_target="tpu_custom_call" | custom-call | tf_op jit(solution)/shard_map/pallas_call | solution.py:357

commit v3 on v2

--- a/solution.py
+++ b/solution.py
@@ -188,19 +188,37 @@
 
     for spot, step in enumerate(order):
         term(own, spot, partner(outer, n_outer, step), inner)
+    last = n_outer - 1
+    relayed = n_outer == 4
+    inside = lax.rem(lax.div(outer, 2) + lax.rem(outer, 2), 2)
     far = []
     for spot, step in enumerate(order):
         near[spot].wait_recv()
-        if step:
-            own[spot] = own[spot] + near_recv[spot]
-            each = copy(
-                own.at[spot], far_recv.at[spot], fs_s.at[spot], fs_r.at[spot],
-                (2 * partner(outer, n_outer, step) + inner, mp),
-            )
-            each.start()
-            far.append(each)
-    last = n_outer - 1
-    total = own[last] + near_recv[last]
+        if not step:
+            continue
+        own[spot] = own[spot] + near_recv[spot]
+        where = spot
+        target = partner(outer, n_outer, step)
+        if relayed and spot == 0:
+            where = last * (1 - inside)
+            aside = partner(outer, n_outer, 1)
+            target = aside + inside * (target - aside)
+        if relayed and spot == 1:
+
+            @pl.when(inside == 1)
+            def _():
+                copy(
+                    own.at[0], far_recv.at[last], fs_s.at[0], fs_r.at[last], (dp, mp)
+                ).wait_recv()
+                own[1] = own[1] + far_recv[last]
+
+        each = copy(
+            own.at[spot], far_recv.at[where], fs_s.at[spot], fs_r.at[where],
+            (2 * target + inner, mp),
+        )
+        each.start()
+        far.append(each)
+    own[last] = own[last] + near_recv[last]
 
     for each in peak_copies:
         each.wait_recv()
@@ -215,7 +233,15 @@
         each.start()
         peak2_copies.append(each)
 
-    for spot in range(last):
+    if relayed:
+
+        @pl.when(inside == 1)
+        def _():
+            copy(own.at[0], far_recv.at[0], fs_s.at[0], fs_r.at[0], (dp, mp)).wait_recv()
+            own[last] = own[last] + far_recv[0]
+
+    total = own[last]
+    for spot in range(1 if relayed else 0, last):
         far[spot].wait_recv()
         total = total + far_recv[spot]
     for each in loads[8:]:

time: 33.8 us -> 33.4 us (0.988); the launches traced: 33.3 us -> 33.3 us
  no operation moved by 1% of the time
where the time goes in v3:
time: 33.4 us; the launch traced here: 33.3 us
  Pallas kernels  32.6 us (98%)
  between operations  0.64 us (2%)
    pallas_call x1, Pallas kernels, local(): pl.pallas_call(functools.partial(kernel, n_dp, n_mp, heads), out_shape=[v...  31.7 us
    pallas_call x1, Pallas kernels, local(): pl.pallas_call(functools.partial(finish, n_mp), out_shape=[jax.ShapeDtype...  0.9 us

profile of v3, /device:TPU:0, one launch (start us, length us, event | category | flops | bytes accessed | tf_op | source)
XLA Modules:
  0.0 33.3 jit_solution(944135727691630742)
XLA Ops:
  0.6 31.7 %shard_map.147 = (f32[1,192,128]{2,1,0:T(8,128)S(1)}, f32[1,64,128]{2,1,0:T(8,128)S(1)}, f32[1,192,128]{2,1,0:T(8,128)S(1)}, f32[1,64,128]{2,1,0:T(8,128)S(1)}, ...) custom-call(bf16[2,192,256]{2,1,0:T(8,128)(2,1)} %bitcast.4, bf16[2,64,256]{2,1,0:T(8,128)(2,1)} %bitcast.5, ...), custom_call_target="tpu_custom_call" | custom-call | tf_op jit(solution)/shard_map/pallas_call | solution.py:349
  32.4 0.9 %shard_map.148 = (f32[1,192,128]{2,1,0:T(8,128)}, f32[1,64,128]{2,1,0:T(8,128)}, f32[1,192,128]{2,1,0:T(8,128)}, f32[1,64,128]{2,1,0:T(8,128)}) custom-call(f32[1,192,128]{2,1,0:T(8,128)S(1)} %get-tuple-element.10.qw_ref, f32[1,64,128]{2,1,0:T(8,128)S(1)} %get-tuple-element.11.kw_ref, f32[1,192,128]{2,1,0:T(8,128)S(1)} %get-tuple-element.12.qm_ref, ...), custom_call_target="tpu_custom_call" | custom-call | tf_op jit(solution)/shard_map/pallas_call | solution.py:383

commit v4 on v3

--- a/solution.py
+++ b/solution.py
@@ -97,8 +97,8 @@
     qw_out, kw_out, qm_out, km_out, mix, shrink_out,
     ql_ref, kl_ref, qg_ref, kg_ref, qh_ref, kh_ref, qp_ref, kp_ref, qw_ref, kw_ref, qm_ref, km_ref, in_sems,
     near_send, near_recv, own, far_recv, peak_send, peak_recv, peak2_send, peak2_recv,
-    grams, gram_recv, row_send, row_recv, z_send, z_recv,
-    ns_s, ns_r, fs_s, fs_r, pk_s, pk_r, pm_s, pm_r, g_s, g_r, y_s, y_r, z_s, z_r, m_s, m_r,
+    grams, gram_recv, row_send, row_recv,
+    ns_s, ns_r, fs_s, fs_r, pk_s, pk_r, pm_s, pm_r, g_s, g_r, y_s, y_r, m_s, m_r,
 ):
     dp = lax.axis_index("dp")
     mp = lax.axis_index("mp")
@@ -119,6 +119,12 @@
         pl.semaphore_signal(
             barrier, inc=1, device_id=(lax.rem(dp + step, n_dp), mp), device_id_type=MESH
         )
+    def owner(step):
+        across = lax.rem(dp + (step // n_group) * heads, n_dp)
+        return across, 2 * lax.rem(group + step, n_group) + core
+
+    for step in range(n_group + 1, 2 * n_group):
+        pl.semaphore_signal(barrier, inc=1, device_id=owner(step), device_id_type=MESH)
     for step in range(1, n_mp):
         pl.semaphore_signal(
             barrier, inc=1, device_id=(dp, lax.rem(mp + step, n_mp)), device_id_type=MESH
@@ -156,7 +162,7 @@
     for spot, step in enumerate(order):
         term(near_send, spot, partner(outer, n_outer, step), 1 - inner)
         if spot == 0:
-            pl.semaphore_wait(barrier, n_dp + n_mp - 2)
+            pl.semaphore_wait(barrier, n_dp + n_mp + n_group - 3)
         each = copy(near_send.at[spot], near_recv.at[spot], ns_s.at[spot], ns_r.at[spot], neighbour)
         each.start()
         near.append(each)
@@ -260,24 +266,17 @@
     swap.start()
     swap.wait_recv()
     whole = grams[core] + gram_recv[...]
+    row_send[...] = whole
     rows = []
-    if n_group > 1:
-        row_send[...] = whole
-        for step in range(1, n_group):
-            each = copy(
-                row_send, row_recv.at[step - 1], y_s.at[step - 1], y_r.at[step - 1],
-                (dp, 2 * lax.rem(group + step, n_group) + core),
-            )
-            each.start()
-            rows.append(each)
-        for step in range(1, n_group):
-            rows[step - 1].wait_recv()
-            whole = whole + row_recv[step - 1]
-    z_send[...] = whole
-    cross = copy(z_send, z_recv, z_s, z_r, (lax.rem(dp + heads, n_dp), mp))
-    cross.start()
-    cross.wait_recv()
-    whole = unfold(whole + z_recv[...])
+    for step in range(1, 2 * n_group):
+        each = copy(
+            row_send, row_recv.at[step - 1], y_s.at[step - 1], y_r.at[step - 1], owner(step)
+        )
+        each.start()
+        rows.append(each)
+    for each in rows:
+        each.wait_recv()
+    whole = unfold(whole + jnp.sum(row_recv[...], axis=0))
 
     eye = (
         lax.broadcasted_iota(jnp.int32, (width, width), 0)
@@ -310,7 +309,7 @@
     qw_out[0] = (qw_ref[0] * keep) * shrink
     kw_out[0] = (kw_ref[0] * keep) * shrink
     swap2.wait_recv()
-    for each in near + far + peak_copies + peak2_copies + [swap] + rows + [cross, swap2]:
+    for each in near + far + peak_copies + peak2_copies + [swap] + rows + [swap2]:
         each.wait_send()
 
 
@@ -332,7 +331,7 @@
     n_mp = lax.axis_size("mp")
     heads = n_dp // 2
     n_outer = n_dp // 2
-    n_group = max(n_mp // 2, 2)
+    n_group = n_mp // 2
     rows = q_latent.shape[2] + kv_latent.shape[2]
     width = q_moment.shape[2]
     operands = (
@@ -364,16 +363,13 @@
             vmem((2,) + folded, F32),
             vmem(folded, F32),
             vmem(folded, F32),
-            vmem((n_group - 1,) + folded, F32),
-            vmem(folded, F32),
-            vmem(folded, F32),
+            vmem((2 * n_group - 1,) + folded, F32),
             dma((n_outer,)), dma((n_outer,)),
             dma((n_outer,)), dma((n_outer,)),
             dma((n_dp - 1,)), dma((n_dp - 1,)),
             dma((n_mp - 1,)), dma((n_mp - 1,)),
             dma, dma,
-            dma((n_group - 1,)), dma((n_group - 1,)),
-            dma, dma,
+            dma((2 * n_group - 1,)), dma((2 * n_group - 1,)),
             dma, dma,
         ],
         compiler_params=pltpu.CompilerParams(

time: 33.4 us -> 32.2 us (0.964)
  Pallas kernels: 32.6 us -> 31.4 us
    pallas_call x1, Pallas kernels: 31.7 us -> 30.5 us  [local(): pl.pallas_call(functools.partial(kernel, n_dp, n_mp, heads), out_shape=[v...]
where the time goes in v4:
time: 32.2 us; the launch traced here: 32 us
  Pallas kernels  31.4 us (98%)
  between operations  0.64 us (2%)
    pallas_call x1, Pallas kernels, local(): pl.pallas_call(functools.partial(kernel, n_dp, n_mp, heads), out_shape=[v...  30.5 us
    pallas_call x1, Pallas kernels, local(): pl.pallas_call(functools.partial(finish, n_mp), out_shape=[jax.ShapeDtype...  0.9 us

profile of v4, /device:TPU:0, one launch (start us, length us, event | category | flops | bytes accessed | tf_op | source)
XLA Modules:
  0.0 32.0 jit_solution(12918884831889103072)
XLA Ops:
  0.6 30.5 %shard_map.147 = (f32[1,192,128]{2,1,0:T(8,128)S(1)}, f32[1,64,128]{2,1,0:T(8,128)S(1)}, f32[1,192,128]{2,1,0:T(8,128)S(1)}, f32[1,64,128]{2,1,0:T(8,128)S(1)}, ...) custom-call(bf16[2,192,256]{2,1,0:T(8,128)(2,1)} %bitcast.4, bf16[2,64,256]{2,1,0:T(8,128)(2,1)} %bitcast.5, ...), custom_call_target="tpu_custom_call" | custom-call | tf_op jit(solution)/shard_map/pallas_call | solution.py:348
  31.1 0.9 %shard_map.148 = (f32[1,192,128]{2,1,0:T(8,128)}, f32[1,64,128]{2,1,0:T(8,128)}, f32[1,192,128]{2,1,0:T(8,128)}, f32[1,64,128]{2,1,0:T(8,128)}) custom-call(f32[1,192,128]{2,1,0:T(8,128)S(1)} %get-tuple-element.10.qw_ref, f32[1,64,128]{2,1,0:T(8,128)S(1)} %get-tuple-element.11.kw_ref, f32[1,192,128]{2,1,0:T(8,128)S(1)} %get-tuple-element.12.qm_ref, ...), custom_call_target="tpu_custom_call" | custom-call | tf_op jit(solution)/shard_map/pallas_call | solution.py:379

commit v5 on v4

--- a/solution.py
+++ b/solution.py
@@ -33,7 +33,9 @@
 
 
 def mm3(a, b):
-    return mm(a[0], b[0]) + (mm(a[0], b[1]) + mm(a[1], b[0]))
+    both = mm(a[0], jnp.concatenate([b[0], b[1]], axis=1))
+    width = b[0].shape[1]
+    return both[:, :width] + (both[:, width:] + mm(a[1], b[0]))
 
 
 def gram(rows):
@@ -114,22 +116,6 @@
     tokens = qg_ref.shape[0]
     other_core = mp + 1 - 2 * core
 
-    barrier = pltpu.get_barrier_semaphore()
-    for step in range(1, n_dp):
-        pl.semaphore_signal(
-            barrier, inc=1, device_id=(lax.rem(dp + step, n_dp), mp), device_id_type=MESH
-        )
-    def owner(step):
-        across = lax.rem(dp + (step // n_group) * heads, n_dp)
-        return across, 2 * lax.rem(group + step, n_group) + core
-
-    for step in range(n_group + 1, 2 * n_group):
-        pl.semaphore_signal(barrier, inc=1, device_id=owner(step), device_id_type=MESH)
-    for step in range(1, n_mp):
-        pl.semaphore_signal(
-            barrier, inc=1, device_id=(dp, lax.rem(mp + step, n_mp)), device_id_type=MESH
-        )
-
     loads = [
         pltpu.make_async_copy(src, dst, in_sems.at[i])
         for i, (src, dst) in enumerate((
@@ -140,6 +126,22 @@
     ]
     for each in loads:
         each.start()
+
+    barrier = pltpu.get_barrier_semaphore()
+    for step in range(1, n_dp):
+        pl.semaphore_signal(
+            barrier, inc=1, device_id=(lax.rem(dp + step, n_dp), mp), device_id_type=MESH
+        )
+    def owner(step):
+        across = lax.rem(dp + (step // n_group) * heads, n_dp)
+        return across, 2 * lax.rem(group + step, n_group) + core
+
+    for step in range(n_group + 1, 2 * n_group):
+        pl.semaphore_signal(barrier, inc=1, device_id=owner(step), device_id_type=MESH)
+    for step in range(1, n_mp):
+        pl.semaphore_signal(
+            barrier, inc=1, device_id=(dp, lax.rem(mp + step, n_mp)), device_id_type=MESH
+        )
 
     def copy(src, dst, send, recv, where):
         return pltpu.make_async_remote_copy(
@@ -274,6 +276,16 @@
         )
         each.start()
         rows.append(each)
+    for each in peak2_copies:
+        each.wait_recv()
+    peaks = jnp.maximum(peaks, jnp.max(peak2_recv[...], axis=0))
+    mine = jnp.where(lane == lax.rem(dp, heads), peaks, LOWEST)
+    peak = jnp.max(jnp.max(mine, axis=0, keepdims=True), axis=1, keepdims=True)
+    shrink = jnp.sqrt(CLIP_LEVEL / jnp.maximum(peak, CLIP_LEVEL))
+    keep = 1.0 - STEP_SIZE * DECAY
+    shrink_out[...] = jnp.broadcast_to(shrink, shrink_out.shape)
+    qw_out[0] = (qw_ref[0] * keep) * shrink
+    kw_out[0] = (kw_ref[0] * keep) * shrink
     for each in rows:
         each.wait_recv()
     whole = unfold(whole + jnp.sum(row_recv[...], axis=0))
@@ -298,16 +310,6 @@
     swap2 = copy(mix.at[core], mix.at[core], m_s, m_r, (dp, other_core))
     swap2.start()
 
-    for each in peak2_copies:
-        each.wait_recv()
-    peaks = jnp.maximum(peaks, jnp.max(peak2_recv[...], axis=0))
-    mine = jnp.where(lane == lax.rem(dp, heads), peaks, LOWEST)
-    peak = jnp.max(jnp.max(mine, axis=0, keepdims=True), axis=1, keepdims=True)
-    shrink = jnp.sqrt(CLIP_LEVEL / jnp.maximum(peak, CLIP_LEVEL))
-    keep = 1.0 - STEP_SIZE * DECAY
-    shrink_out[...] = jnp.broadcast_to(shrink, shrink_out.shape)
-    qw_out[0] = (qw_ref[0] * keep) * shrink
-    kw_out[0] = (kw_ref[0] * keep) * shrink
     swap2.wait_recv()
     for each in near + far + peak_copies + peak2_copies + [swap] + rows + [swap2]:
         each.wait_send()

time: 32.2 us -> 32 us (level)
  no operation moved by 1% of the time
where the time goes in v5:
time: 32 us; the launch traced here: 31.8 us
  Pallas kernels  31.2 us (98%)
  between operations  0.64 us (2%)
    pallas_call x1, Pallas kernels, local(): pl.pallas_call(functools.partial(kernel, n_dp, n_mp, heads), out_shape=[v...  30.3 us
    pallas_call x1, Pallas kernels, local(): pl.pallas_call(functools.partial(finish, n_mp), out_shape=[jax.ShapeDtype...  0.9 us

profile of v5, /device:TPU:0, one launch (start us, length us, event | category | flops | bytes accessed | tf_op | source)
XLA Modules:
  0.0 31.8 jit_solution(15580580390361723205)
XLA Ops:
  0.6 30.3 %shard_map.147 = (f32[1,192,128]{2,1,0:T(8,128)S(1)}, f32[1,64,128]{2,1,0:T(8,128)S(1)}, f32[1,192,128]{2,1,0:T(8,128)S(1)}, f32[1,64,128]{2,1,0:T(8,128)S(1)}, ...) custom-call(bf16[2,192,256]{2,1,0:T(8,128)(2,1)} %bitcast.4, bf16[2,64,256]{2,1,0:T(8,128)(2,1)} %bitcast.5, ...), custom_call_target="tpu_custom_call" | custom-call | tf_op jit(solution)/shard_map/pallas_call | solution.py:350
  30.9 0.9 %shard_map.148 = (f32[1,192,128]{2,1,0:T(8,128)}, f32[1,64,128]{2,1,0:T(8,128)}, f32[1,192,128]{2,1,0:T(8,128)}, f32[1,64,128]{2,1,0:T(8,128)}) custom-call(f32[1,192,128]{2,1,0:T(8,128)S(1)} %get-tuple-element.10.qw_ref, f32[1,64,128]{2,1,0:T(8,128)S(1)} %get-tuple-element.11.kw_ref, f32[1,192,128]{2,1,0:T(8,128)S(1)} %get-tuple-element.12.qm_ref, ...), custom_call_target="tpu_custom_call" | custom-call | tf_op jit(solution)/shard_map/pallas_call | solution.py:381
